TPU v7x, 32 devices: a whole 2x2x4 slice. The times are simulated.
32 devices in a mesh: samples: 8 (over z, y), variants: 4 (over x, core).
Axes of the slice: x: 2, y: 2, z: 4, core: 2. Of those that a mesh axis runs over, the one named last changes fastest.
Arguments:
- genotypes: int32 [2048, 32768], P('variants', 'samples'), may hold values from 0 to 3, as said below
- weights: float32 [32768], P('samples'), may hold values from 0.25 to 20
Outputs:
- call_mean: float32 [2048], P('variants')
- call_var: float32 [2048], P('variants')
- class_counts: int32 [4, 2048], P(None, 'variants')
- ld_window: float32 [1024, 2048], P('samples', 'variants')
- sample_calls: int32 [2, 32768], P(None, 'samples')
- sample_share: float32 [32768], P('samples')
Inputs may be any that keep to these rules, and one draw needn't show every extreme that they name: `genotypes`: in every variant's row, each aligned group of 8 samples (samples 8 i to 8 i + 7) holds at least one call other than 3.
All inputs are finite; a program needn't handle non-finite values.
Results may differ from a plain program's by a relative error of at most 0.0004.
Values may be sent and summed in bfloat16 or wider, within the bound.
A program may use at most 64 MiB of HBM per device.

v0:
```python
import jax
import jax.numpy as jnp
from jax import lax
from jax.sharding import PartitionSpec as P


def shifted(value, axis, by):
    size = lax.axis_size(axis)
    pairs = [(i, i + by) for i in range(size) if 0 <= i + by < size]
    return lax.ppermute(value, axis, pairs)


def on_device(genotypes, weights):
    present = genotypes != 3
    called = present.astype(jnp.float32)
    dosage = jnp.where(present, genotypes, 0).astype(jnp.float32)
    weighted = called * weights[None, :]
    w_sum_part = jnp.sum(weighted, axis=1)
    first_part = jnp.sum(weighted * dosage, axis=1)
    classes = jnp.stack(
        [jnp.sum((genotypes == level).astype(jnp.float32), axis=1) for level in range(4)]
    )
    second_part = jnp.sum(weighted * dosage * dosage, axis=1)
    w_sum, first_total, second_total, class_total = lax.psum(
        (w_sum_part, first_part, second_part, classes), "samples"
    )
    mean_value = first_total / w_sum
    deviation = second_total - first_total * mean_value
    var_value = deviation / w_sum
    factor = 1.0 / jnp.sqrt(w_sum * (var_value + 1e-05))
    centered = (dosage - mean_value[:, None]) * called
    scaled = (jnp.sqrt(weights)[None, :] * centered * factor[:, None]).astype(jnp.bfloat16)
    following = shifted(scaled, "variants", -1)
    joined = jnp.concatenate([scaled, following], axis=0)
    rows_owned = joined.shape[0] // lax.axis_size("samples")
    partial_all = lax.dot_general(
        joined, scaled, (((1,), (1,)), ((), ())), preferred_element_type=jnp.float32
    )
    summed = lax.psum(partial_all, "samples")
    ld_window = lax.dynamic_slice_in_dim(
        summed, lax.axis_index("samples") * rows_owned, rows_owned, 0
    )
    squares = scaled.astype(jnp.float32)
    called_total, het_total, square_total = lax.psum(
        (
            jnp.sum(called, axis=0),
            jnp.sum((genotypes == 1).astype(jnp.float32), axis=0),
            jnp.sum(squares * squares, axis=0),
        ),
        "variants",
    )
    samples_all = weights.shape[0] * lax.axis_size("samples")
    variants_all = genotypes.shape[0] * lax.axis_size("variants")
    sample_share = square_total * (samples_all / variants_all)
    sample_calls = jnp.stack([called_total, het_total]).astype(jnp.int32)
    return (
        mean_value,
        var_value,
        class_total.astype(jnp.int32),
        ld_window,
        sample_calls,
        sample_share,
    )


def solution(mesh):
    placed = (P("variants", "samples"), P("samples"))
    return jax.shard_map(
        on_device,
        mesh=mesh,
        in_specs=placed,
        out_specs=(
            P("variants"),
            P("variants"),
            P(None, "variants"),
            P("samples", "variants"),
            P(None, "samples"),
            P("samples"),
        ),
        check_vma=False,
    )
```

profile of v0, /device:TPU:0, one launch (start us, length us, event | category | flops | bytes accessed | tf_op | source)
XLA Modules:
  0.0 226.3 jit_solution(9397429142286188237)
XLA Ops:
  7.2 0.0 copy-start.1
  7.2 0.0 all-reduce.4.cloned.1.call-start
  7.2 0.0 copy-start
  7.2 5.0 %convert_reduce_fusion = (f32[4096]{0:T(1024)S(1)}, f32[512]{0:T(512)S(1)}) fusion(s32[512,4096]{1,0:T(8,128)} %param.2), kind=kLoop, calls=%fused_computation | loop fusion | flops 8384000 | bytes 8407040 | tf_op jit(solution)/shard_map/reduce_sum | solution.py:47
  12.3 0.0 copy-done.1
  12.3 0.7 copy-done
  13.0 6.3 %fusion.2 = (f32[512]{0:T(512)S(1)}, f32[512]{0:T(512)S(1)}, f32[512]{0:T(512)S(1)}, f32[4096]{0:T(1024)S(1)}, f32[512]{0:T(512)S(1)}, /*index=5*/f32[512]{0:T(512)S(1)}, f32[512]{0:T(512)S(1)}) fusion(s32[512,4096]{1,0:T(8,128)S(1)} %copy-done, f32[4096]{0:T(1024)S(1)} %copy-done.1), kind=kLoop, calls=%fused_computation.6 | loop fusion | flops 41935872 | bytes 8433664 | tf_op jit(solution)/shard_map/reduce_sum | solution.py:23
  19.4 38.9 %all-reduce = (f32[512]{0:T(512)S(1)}, f32[512]{0:T(512)S(1)}, f32[512]{0:T(512)S(1)}, f32[4,512]{1,0:T(4,128)S(1)}) all-reduce(f32[512]{0:T(512)S(1)} %get-tuple-element.8, f32[512]{0:T(512)S(1)} %get-tuple-element.7, f32[512]{0:T(512)S(1)} %get-tuple-element.6, ...), channel_id=1, replica_groups=mesh['samples'=8,'variants'=4] {'samples'}, use_global_device_ids=true, to_apply=%region_1.2 | all-reduce | flops 3584 | bytes 28672 | tf_op jit(solution)/shard_map/psum | solution.py:24
  58.2 0.6 multiply_rsqrt_fusion
  58.8 0.0 copy-start.2
  58.8 5.2 %multiply_reduce_fusion = (f32[4096]{0:T(1024)S(1)}, bf16[512,4096]{1,0:T(8,128)(2,1)S(1)}) fusion(f32[512]{0:T(512)S(1)} %get-tuple-element.24, f32[512]{0:T(512)S(1)} %get-tuple-element.26, s32[512,4096]{1,0:T(8,128)} %param.2, f32[4096]{0:T(1024)S(1)} %sqrt.6), kind=kLoop, calls=%fused_computation.11 | loop fusion | flops 23064576 | bytes 12619776 | tf_op jit(solution)/shard_map/reduce_sum | solution.py:48
  64.0 1.3 collective-permute-start
  65.3 7.8 %collective-permute-done = bf16[512,4096]{1,0:T(8,128)(2,1)S(1)} collective-permute-done((bf16[512,4096]{1,0:T(8,128)(2,1)S(1)}, bf16[512,4096]{1,0:T(8,128)(2,1)S(1)}, u32[]{:S(2)}, u32[]{:S(2)}) %collective-permute-start) | collective-permute-done | bytes 4194336 | tf_op jit(solution)/shard_map/ppermute | solution.py:10
  73.1 5.8 %fusion.3 = f32[1024,512]{1,0:T(8,128)} fusion(bf16[512,4096]{1,0:T(8,128)(2,1)S(1)} %get-tuple-element.23, bf16[512,4096]{1,0:T(8,128)(2,1)S(1)} %collective-permute-done), kind=kOutput, calls=%fused_computation.7 | convolution fusion | flops 4311744512 | bytes 10485760 | tf_op jit(solution)/shard_map/dot_general | solution.py:36
  78.9 0.0 copy-done.2
  78.9 0.0 all-reduce.4.cloned.1.call-update
  78.9 0.6 convert_element_type.36
  79.5 51.9 %all-reduce.1 = (f32[1,4096]{1,0:T(1,128)S(1)}, f32[1,4096]{1,0:T(1,128)S(1)}, f32[4096]{0:T(1024)S(1)}) all-reduce(f32[1,4096]{1,0:T(1,128)S(1)} %bitcast.7, f32[1,4096]{1,0:T(1,128)S(1)} %bitcast.8, f32[4096]{0:T(1024)S(1)} %get-tuple-element.22), channel_id=1, replica_groups=mesh['samples'=8,'variants'=4] {'variants'}, use_global_device_ids=true, to_apply=%region_15.16 | all-reduce | flops 12288 | bytes 98304 | tf_op jit(solution)/shard_map/psum | solution.py:44
  131.4 0.6 broadcast_multiply_fusion
  132.0 0.7 maximum_convert_fusion
  132.7 85.1 %all-reduce.4.cloned.1.call-done = f32[1024,512]{1,0:T(8,128)} async-done(((f32[1024,512]{1,0:T(8,128)}), f32[1024,512]{1,0:T(8,128)}) %all-reduce.4.cloned.1.call-update) | async-done | bytes 2097168 | tf_op jit(solution)/shard_map/psum | solution.py:39
  217.8 1.7 constant_dynamic-slice_fusion
  (2 shorter events, 0.0 us)
Async XLA Ops:
  7.2 5.1 %copy-start.1 = (f32[4096]{0:T(1024)S(1)}, f32[4096]{0:T(1024)}, u32[]{:S(2)}) copy-start(f32[4096]{0:T(1024)} %param.3) | copy-start | bytes 49156
  7.2 210.6 %all-reduce.4.cloned.1.call-start = ((), (), s32[]{:S(2)}) async-start(), calls=%async_computation | async-start | bytes 4194304 | tf_op jit(solution)/shard_map/psum | solution.py:39
  7.2 5.8 %copy-start = (s32[512,4096]{1,0:T(8,128)S(1)}, s32[512,4096]{1,0:T(8,128)}, u32[]{:S(2)}) copy-start(s32[512,4096]{1,0:T(8,128)} %param.2) | copy-start | bytes 25165828
  58.8 20.0 %copy-start.2 = (f32[512]{0:T(512)}, f32[512]{0:T(512)S(1)}, u32[]{:S(2)}) copy-start(f32[512]{0:T(512)S(1)} %get-tuple-element.26) | copy-start | bytes 6148
  64.0 9.1 %collective-permute-start = (bf16[512,4096]{1,0:T(8,128)(2,1)S(1)}, bf16[512,4096]{1,0:T(8,128)(2,1)S(1)}, u32[]{:S(2)}, u32[]{:S(2)}) collective-permute-start(bf16[512,4096]{1,0:T(8,128)(2,1)S(1)} %get-tuple-element.23), channel_id=1, source_target_pairs={{1,0},{2,1},{3,2},{5,4},{6,5},{7,6},{9,8},{10,9},{11,10},{13,12},{... | collective-permute-start | bytes 12582920 | tf_op jit(solution)/shard_map/ppermute | solution.py:10
Sparse Core Ops, SparseCore 0:
  79.0 138.7 all-reduce.3
where the time goes:
time: 227 us; the launch traced here: 226 us
  waiting for transfers between devices  92.8 us (41%)
  blocking collectives  90.8 us (40%)
  other arithmetic  19 us (8%)
  between operations  14.1 us (6%)
  matrix products  5.81 us (3%)
  local copies, waits for them, and re-layouts  2.4 us (1%)
    psum x1, waiting for transfers between devices, on_device(): summed = lax.psum(partial_all, 'samples')  85.1 us
    psum x1, blocking collectives, on_device(): lax.psum((jnp.sum(called, axis=0), jnp.sum((genotypes == 1).astype(jnp.fl...  51.9 us
    psum x1, blocking collectives, on_device(): lax.psum((w_sum_part, first_part, second_part, classes), 'samples')  38.9 us
    ppermute x1, waiting for transfers between devices, shifted(): return lax.ppermute(value, axis, pairs)  7.75 us
    reduce_sum x1, other arithmetic, on_device(): second_part = jnp.sum(weighted * dosage * dosage, axis=1)  6.32 us
    dot_general x1, matrix products, on_device(): lax.dot_general(joined, scaled, (((1,), (1,)), ((), ())), preferred_eleme...  5.81 us
    reduce_sum x1, other arithmetic, on_device(): jnp.sum(squares * squares, axis=0)  5.17 us
    reduce_sum x1, other arithmetic, on_device(): jnp.sum((genotypes == 1).astype(jnp.float32), axis=0)  5.04 us
  transfers between devices with their start and end apart: 2, of which 2 were waited for; matrix products, arithmetic and copies ran while one was open for 1% of the time, Pallas kernels for 0%

commit v1 on v0

--- a/solution.py
+++ b/solution.py
@@ -36,7 +36,7 @@
     partial_all = lax.dot_general(
         joined, scaled, (((1,), (1,)), ((), ())), preferred_element_type=jnp.float32
     )
-    summed = lax.psum(partial_all, "samples")
+    summed = jnp.sum(lax.all_gather(partial_all, "samples"), axis=0)
     ld_window = lax.dynamic_slice_in_dim(
         summed, lax.axis_index("samples") * rows_owned, rows_owned, 0
     )

time: 227 us -> 359 us (1.58)
  waiting for transfers between devices: 92.8 us -> 218 us
  other arithmetic: 19 us -> 27.1 us
    all_gather x0 -> x1, waiting for transfers between devices: none -> 210 us  [on_device(): summed = jnp.sum(lax.all_gather(partial_all, 'samples'), axis=0)]
    psum x1 -> x0, waiting for transfers between devices: 85.1 us -> none  [on_device(): summed = lax.psum(partial_all, 'samples')]
    reduce_sum x0 -> x1, other arithmetic: none -> 8.08 us  [on_device(): summed = jnp.sum(lax.all_gather(partial_all, 'samples'), axis=0)]
where the time goes in v1:
time: 359 us; the launch traced here: 358 us
  waiting for transfers between devices  218 us (61%)
  blocking collectives  90.4 us (25%)
  other arithmetic  27.1 us (8%)
  between operations  14.1 us (4%)
  matrix products  5.87 us (2%)
    all_gather x1, waiting for transfers between devices, on_device(): summed = jnp.sum(lax.all_gather(partial_all, 'samples'), axis=0)  210 us
    psum x1, blocking collectives, on_device(): lax.psum((jnp.sum(called, axis=0), jnp.sum((genotypes == 1).astype(jnp.fl...  51.5 us
    psum x1, blocking collectives, on_device(): lax.psum((w_sum_part, first_part, second_part, classes), 'samples')  38.9 us
    reduce_sum x1, other arithmetic, on_device(): summed = jnp.sum(lax.all_gather(partial_all, 'samples'), axis=0)  8.08 us
    ppermute x1, waiting for transfers between devices, shifted(): return lax.ppermute(value, axis, pairs)  7.75 us
  transfers between devices with their start and end apart: 2, of which 2 were waited for; matrix products, arithmetic and copies ran while one was open for 1% of the time, Pallas kernels for 0%

profile of v1, /device:TPU:0, one launch (start us, length us, event | category | flops | bytes accessed | tf_op | source)
XLA Modules:
  0.0 358.5 jit_solution(4264397444789731672)
XLA Ops:
  7.2 0.0 copy-start.1
  7.2 0.0 all-gather.3.cloned.1.call-start
  7.2 0.0 copy-start
  7.2 5.0 %convert_reduce_fusion = (f32[4096]{0:T(1024)S(1)}, f32[512]{0:T(512)S(1)}) fusion(s32[512,4096]{1,0:T(8,128)} %param.2), kind=kLoop, calls=%fused_computation | loop fusion | flops 8384000 | bytes 8407040 | tf_op jit(solution)/shard_map/reduce_sum | solution.py:47
  12.3 0.0 copy-done.1
  12.3 0.7 copy-done
  13.0 6.3 %fusion.2 = (f32[512]{0:T(512)S(1)}, f32[512]{0:T(512)S(1)}, f32[512]{0:T(512)S(1)}, f32[4096]{0:T(1024)S(1)}, f32[512]{0:T(512)S(1)}, /*index=5*/f32[512]{0:T(512)S(1)}, f32[512]{0:T(512)S(1)}) fusion(s32[512,4096]{1,0:T(8,128)S(1)} %copy-done, f32[4096]{0:T(1024)S(1)} %copy-done.1), kind=kLoop, calls=%fused_computation.6 | loop fusion | flops 41935872 | bytes 8433664 | tf_op jit(solution)/shard_map/reduce_sum | solution.py:23
  19.4 38.9 %all-reduce = (f32[512]{0:T(512)S(1)}, f32[512]{0:T(512)S(1)}, f32[512]{0:T(512)S(1)}, f32[4,512]{1,0:T(4,128)S(1)}) all-reduce(f32[512]{0:T(512)S(1)} %get-tuple-element.8, f32[512]{0:T(512)S(1)} %get-tuple-element.7, f32[512]{0:T(512)S(1)} %get-tuple-element.6, ...), channel_id=1, replica_groups=mesh['samples'=8,'variants'=4] {'samples'}, use_global_device_ids=true, to_apply=%region_1.2 | all-reduce | flops 3584 | bytes 28672 | tf_op jit(solution)/shard_map/psum | solution.py:24
  58.2 0.6 multiply_rsqrt_fusion
  58.8 0.0 copy-start.2
  58.8 5.2 %multiply_reduce_fusion = (f32[4096]{0:T(1024)S(1)}, bf16[512,4096]{1,0:T(8,128)(2,1)S(1)}) fusion(f32[512]{0:T(512)S(1)} %get-tuple-element.24, f32[512]{0:T(512)S(1)} %get-tuple-element.26, s32[512,4096]{1,0:T(8,128)} %param.2, f32[4096]{0:T(1024)S(1)} %sqrt.6), kind=kLoop, calls=%fused_computation.11 | loop fusion | flops 23064576 | bytes 12619776 | tf_op jit(solution)/shard_map/reduce_sum | solution.py:48
  64.0 1.3 collective-permute-start
  65.3 7.8 %collective-permute-done = bf16[512,4096]{1,0:T(8,128)(2,1)S(1)} collective-permute-done((bf16[512,4096]{1,0:T(8,128)(2,1)S(1)}, bf16[512,4096]{1,0:T(8,128)(2,1)S(1)}, u32[]{:S(2)}, u32[]{:S(2)}) %collective-permute-start) | collective-permute-done | bytes 4194336 | tf_op jit(solution)/shard_map/ppermute | solution.py:10
  73.1 5.9 %fusion.3 = f32[1024,512]{1,0:T(8,128)} fusion(bf16[512,4096]{1,0:T(8,128)(2,1)S(1)} %get-tuple-element.23, bf16[512,4096]{1,0:T(8,128)(2,1)S(1)} %collective-permute-done), kind=kOutput, calls=%fused_computation.7 | convolution fusion | flops 4311744512 | bytes 10485760 | tf_op jit(solution)/shard_map/dot_general | solution.py:36
  78.9 0.0 copy-done.2
  78.9 0.0 all-gather.3.cloned.1.call-update
  78.9 0.6 convert_element_type.36
  79.6 51.5 %all-reduce.1 = (f32[1,4096]{1,0:T(1,128)S(1)}, f32[1,4096]{1,0:T(1,128)S(1)}, f32[4096]{0:T(1024)S(1)}) all-reduce(f32[1,4096]{1,0:T(1,128)S(1)} %bitcast.9, f32[1,4096]{1,0:T(1,128)S(1)} %bitcast.10, f32[4096]{0:T(1024)S(1)} %get-tuple-element.22), channel_id=1, replica_groups=mesh['samples'=8,'variants'=4] {'variants'}, use_global_device_ids=true, to_apply=%region_15.16 | all-reduce | flops 12288 | bytes 98304 | tf_op jit(solution)/shard_map/psum | solution.py:44
  131.1 0.6 broadcast_multiply_fusion
  131.7 0.7 maximum_convert_fusion
  132.4 210.4 %all-gather.3.cloned.1.call-done = f32[8192,512]{1,0:T(8,128)} async-done(((f32[1024,512]{1,0:T(8,128)}), f32[8192,512]{1,0:T(8,128)}) %all-gather.3.cloned.1.call-update) | async-done | bytes 16777232 | tf_op jit(solution)/shard_map/all_gather | solution.py:39
  342.8 8.1 %reduce_sum.106 = f32[1024,512]{1,0:T(8,128)S(1)} reduce(f32[8,1024,512]{2,1,0:T(8,128)} %bitcast.8, f32[]{:T(128)} %constant.12.clone.1), dimensions={0}, to_apply=%region_11.12 | reduce | flops 3670016 | bytes 18874372 | tf_op jit(solution)/shard_map/reduce_sum | solution.py:39
  350.9 0.7 constant_dynamic-slice_fusion
  (2 shorter events, 0.0 us)
Async XLA Ops:
  7.2 5.1 %copy-start.1 = (f32[4096]{0:T(1024)S(1)}, f32[4096]{0:T(1024)}, u32[]{:S(2)}) copy-start(f32[4096]{0:T(1024)} %param.3) | copy-start | bytes 49156
  7.2 335.6 %all-gather.3.cloned.1.call-start = ((), (), s32[]{:S(2)}) async-start(), calls=%async_computation | async-start | bytes 18874368 | tf_op jit(solution)/shard_map/all_gather | solution.py:39
  7.2 5.8 %copy-start = (s32[512,4096]{1,0:T(8,128)S(1)}, s32[512,4096]{1,0:T(8,128)}, u32[]{:S(2)}) copy-start(s32[512,4096]{1,0:T(8,128)} %param.2) | copy-start | bytes 25165828
  58.8 20.1 %copy-start.2 = (f32[512]{0:T(512)}, f32[512]{0:T(512)S(1)}, u32[]{:S(2)}) copy-start(f32[512]{0:T(512)S(1)} %get-tuple-element.26) | copy-start | bytes 6148
  64.0 9.1 %collective-permute-start = (bf16[512,4096]{1,0:T(8,128)(2,1)S(1)}, bf16[512,4096]{1,0:T(8,128)(2,1)S(1)}, u32[]{:S(2)}, u32[]{:S(2)}) collective-permute-start(bf16[512,4096]{1,0:T(8,128)(2,1)S(1)} %get-tuple-element.23), channel_id=1, source_target_pairs={{1,0},{2,1},{3,2},{5,4},{6,5},{7,6},{9,8},{10,9},{11,10},{13,12},{... | collective-permute-start | bytes 12582920 | tf_op jit(solution)/shard_map/ppermute | solution.py:10
Sparse Core Ops, SparseCore 0:
  79.1 263.6 all-gather.2
